TPU v7x, 32 devices: a whole 2x2x4 slice. The times are simulated.
32 devices in a mesh: tab: 2 (over x), cand: 4 (over z), dp: 4 (over y, core).
Axes of the slice: x: 2, y: 2, z: 4, core: 2. Of those that a mesh axis runs over, the one named last changes fastest.
Arguments:
- tables: bfloat16 [16, 65536, 128], P(('cand', 'dp'), 'tab'), may hold values from -6 to 6
- bag_ids: int32 [16, 1024, 16], P(('cand', 'dp')), may hold values from 0 to 65535
- bag_lengths: int32 [16, 1024], P(('cand', 'dp')), may hold values from 1 to 16
- item_weight: bfloat16 [2048, 256], replicated, may hold values from -0.125 to 0.125
- user_features: bfloat16 [16384, 512], P(('tab', 'dp')), may hold values from -6 to 6
- user_w1: bfloat16 [512, 1024], replicated, may hold values from -0.25 to 0.25
- user_w2: bfloat16 [1024, 256], replicated, may hold values from -0.1875 to 0.1875
- positive_items: int32 [16384], P(('tab', 'dp')), may hold values from 0 to 1023
Outputs:
- item_emb: float32 [1024, 256], P(('tab', 'cand', 'dp'))
- user_loss: float32 [16384], P(('tab', 'dp'))
Inputs may be any that keep to these rules, and one draw needn't show every extreme that they name: `bag_ids`: row ids of a table. Only the first bag_lengths ids of a bag count; the rest is padding.
All inputs are finite; a program needn't handle non-finite values.
Results may differ from a plain program's by a relative error of at most 0.00046.
Values sent between devices are 32-bit elements; how exact they have to be, the bound alone decides.
A program may use at most 64 MiB of HBM per device.

v0:
```python
import jax
import jax.numpy as jnp
from jax import lax
from jax.sharding import PartitionSpec as P

epsilon = 1e-06
logit_scale = 20.0


def unit_rows(vectors):
    return vectors * lax.rsqrt(jnp.mean(vectors * vectors, axis=-1, keepdims=True) + epsilon)


def lookup_pool(bag_part, length_part, table, row_base):
    rows_total = table.shape[0]
    local = bag_part - row_base
    inside = (local >= 0) & (local < rows_total)
    valid = lax.broadcasted_iota(jnp.int32, bag_part.shape, 1) < length_part[:, None]
    keeping = inside & valid
    picked = jnp.take(table, jnp.clip(local, 0, rows_total - 1), axis=0).astype(jnp.float32)
    summed = jnp.sum(jnp.where(keeping[:, :, None], picked, jnp.float32(0.0)), axis=1)
    return summed / length_part[:, None].astype(jnp.float32)


def user_tower(features, user_w1, user_w2):
    user_hidden = jax.nn.gelu(
        jnp.dot(features, user_w1, preferred_element_type=jnp.float32), approximate=False
    ).astype(jnp.bfloat16)
    return unit_rows(jnp.dot(user_hidden, user_w2, preferred_element_type=jnp.float32))


def body(
    tables, bag_ids, bag_lengths, item_weight, user_features, user_w1, user_w2, positive_items
):
    table = tables[0]
    own_ids = bag_ids[0]
    own_lengths = bag_lengths[0]
    num_cand = lax.axis_size("cand")
    num_dp = lax.axis_size("dp")
    width = table.shape[1]
    embed = item_weight.shape[1]
    table_count = item_weight.shape[0] // width
    row_base = lax.axis_index("tab") * table.shape[0]
    pooled = lax.psum_scatter(
        lookup_pool(own_ids, own_lengths, table, row_base), "tab", scatter_dimension=0, tiled=True
    )
    groups = num_cand * num_dp
    shaped = pooled.reshape(1, groups, pooled.shape[0] // groups, width)
    weight_blocks = item_weight.astype(jnp.float32).reshape(table_count, width, embed)
    stacked = lax.all_to_all(shaped, ("cand", "dp"), split_axis=1, concat_axis=0, tiled=True)[:, 0]
    item_pre = jnp.einsum(
        "fbe,feh->bh",
        stacked,
        weight_blocks,
        precision=lax.Precision.HIGHEST,
        preferred_element_type=jnp.float32,
    )
    item_emb = unit_rows(item_pre)
    scale = logit_scale / embed
    per_block = item_emb.shape[0]
    cand_index = lax.axis_index("cand")

    def make_adder(user_emb, positives):

        def add_scores(carry, piece, global_id):
            scores = (
                lax.dot_general(
                    user_emb,
                    piece,
                    (((1,), (1,)), ((), ())),
                    precision=lax.Precision.HIGHEST,
                    preferred_element_type=jnp.float32,
                )
                * scale
            )
            sums = jnp.sum(jnp.exp(scores), axis=1)
            positive = jnp.sum(
                jnp.where(global_id == positives[:, None], scores, jnp.float32(0.0)), axis=1
            )
            return (sums, positive)

        return add_scores

    user_emb = user_tower(user_features, user_w1, user_w2)
    users_here = user_emb.shape[0]
    start_carry = (jnp.zeros((users_here,), jnp.float32), jnp.zeros((users_here,), jnp.float32))
    add_scores = make_adder(user_emb, positive_items)
    piece = lax.all_gather(item_emb, ("tab", "dp"), axis=0, tiled=True)
    place = lax.broadcasted_iota(jnp.int32, (1, piece.shape[0]), 1)
    group = place // per_block
    within = place % per_block
    global_id = (
        (group // num_dp * num_cand + cand_index) * num_dp + group % num_dp
    ) * per_block + within
    partial_sums = add_scores(start_carry, piece, global_id)
    sums, positive = lax.psum((partial_sums[0], partial_sums[1]), "cand")
    user_loss = jnp.log(sums) - positive
    return (item_emb, user_loss)


def solution(mesh):
    placed = (
        P(("cand", "dp"), "tab", None),
        P(("cand", "dp"), None, None),
        P(("cand", "dp"), None),
        P(),
        P(("tab", "dp"), None),
        P(),
        P(),
        P(("tab", "dp")),
    )
    return jax.shard_map(
        body,
        mesh=mesh,
        in_specs=placed,
        out_specs=(P(("tab", "cand", "dp"), None), P(("tab", "dp"))),
        check_vma=False,
    )
```

profile of v0, /device:TPU:0, one launch (start us, length us, event | category | flops | bytes accessed | tf_op | source)
XLA Modules:
  0.0 165.8 jit_solution(16034018554807832179)
XLA Ops:
  7.2 0.0 copy-start
  7.2 0.0 reduce-scatter.2.cloned.1.call-start
  7.2 1.0 compare_select_fusion
  8.2 0.9 fusion.17
  9.1 0.7 convert_element_type.16
  9.8 0.3 copy.15
  10.1 0.3 copy.16
  10.4 0.2 copy.17
  10.6 0.2 reshape.227
  10.8 59.4 %gather_fusion = bf16[16384,128]{1,0:T(8,128)(2,1)} fusion(bf16[32768,128]{1,0:T(8,128)(2,1)} %bitcast.28, s32[16384]{0:T(1024)S(1)} %broadcast_clamp_fusion), kind=kCustom, calls=%fused_computation | custom fusion | bytes 8454144 | tf_op jit(solution)/shard_map/jit(_take)/gather | solution.py:20
  70.2 7.2 %select_reduce_fusion = f32[1024,128]{1,0:T(8,128)S(1)} fusion(pred[1024,16]{1,0:T(8,128)(4,1)S(1)} %copy.16, pred[1024,16]{1,0:T(8,128)(4,1)S(1)} %copy.15, bf16[16384,128]{1,0:T(8,128)(2,1)} %gather_fusion), kind=kLoop, calls=%fused_computation.18 | loop fusion | flops 8257536 | bytes 4751360 | tf_op jit(solution)/shard_map/reduce_sum | solution.py:21
  77.4 1.0 broadcast_divide_fusion
  78.4 0.0 reduce-scatter.2.cloned.1.call-update
  78.4 17.5 %reduce-scatter.2.cloned.1.call-done = f32[512,128]{1,0:T(8,128)} async-done(((f32[1024,128]{1,0:T(8,128)}), f32[512,128]{1,0:T(8,128)}) %reduce-scatter.2.cloned.1.call-update) | async-done | bytes 262160 | tf_op jit(solution)/shard_map/reduce_scatter | solution.py:44
  95.9 5.8 %all-to-all-start = ((f32[1,16,32,128]{3,2,0,1:T(8,128)}), f32[1,16,32,128]{3,2,0,1:T(8,128)S(1)}, u32[]{:S(2)}, u32[]{:S(2)}) async-start(f32[1,16,32,128]{3,2,0,1:T(8,128)} %bitcast.30), calls=%async_computation.1 | async-start | bytes 524288 | tf_op jit(solution)/shard_map/all_to_all | solution.py:50
  101.7 0.0 copy-done
  101.7 0.0 copy-start.1
  101.7 0.0 copy-start.3
  101.7 23.2 %multiply_reduce_fusion = (f32[2048]{0:T(1024)S(1)}, f32[2048,256]{0,1:T(8,128)}) fusion(bf16[1024,256]{1,0:T(8,128)(2,1)} %param.14, bf16[2048,512]{1,0:T(8,128)(2,1)S(1)} %copy-done, bf16[512,1024]{1,0:T(8,128)(2,1)} %param.13), kind=kOutput, calls=%fused_computation.27 | convolution fusion | flops 3358586880 | bytes 5775360 | tf_op jit(solution)/shard_map/dot_general | solution.py:29
  125.0 0.0 all-to-all-done
  125.0 0.0 copy-done.1
  125.0 0.7 multiply_reduce_fusion.1
  125.7 0.1 broadcast_multiply_fusion
  125.8 0.0 copy-start.2
  125.8 9.8 %all_gather.3 = f32[256,256]{1,0:T(8,128)S(1)} all-gather(f32[32,256]{1,0:T(8,128)S(1)} %broadcast_multiply_fusion), channel_id=1, replica_groups=mesh['tab'=2,'cand'=4,'dp'=4] {'tab','dp'}, dimensions={0}, use_global_device_ids=true | all-gather | bytes 294912 | tf_op jit(solution)/shard_map/all_gather | solution.py:88
  135.6 0.0 copy-done.3
  135.6 4.1 %exponential_reduce_fusion = (f32[2048]{0:T(1024)S(1)}, f32[2048]{0:T(1024)S(1)}) fusion(s32[2048]{0:T(1024)S(1)} %copy-done.3, s32[256]{0:T(256)S(1)} %fusion.20, f32[256,256]{1,0:T(8,128)S(1)} %all_gather.3, f32[2048,256]{0,1:T(8,128)} %get-tuple-element.11, f32[2048]{0:T(1024)S(1)} %add_rsqrt_fusion), kind=kOutput, calls=%fused_computation.25 | convolution fusion | flops 1613754368 | bytes 2393088 | tf_op jit(solution)/shard_map/dot_general | solution.py:67
  139.7 18.7 %all-reduce = (f32[2048]{0:T(1024)S(1)}, f32[2048]{0:T(1024)S(1)}) all-reduce(f32[2048]{0:T(1024)S(1)} %get-tuple-element.3, f32[2048]{0:T(1024)S(1)} %get-tuple-element.2), channel_id=1, replica_groups=mesh['tab'=2,'cand'=4,'dp'=4] {'cand'}, use_global_device_ids=true, to_apply=%region_7.8 | all-reduce | flops 4096 | bytes 32768 | tf_op jit(solution)/shard_map/psum | solution.py:96
  158.4 0.6 log_subtract_fusion
  159.0 0.0 copy-done.2
  (4 shorter events, 0.0 us)
Async XLA Ops:
  7.2 94.6 %copy-start = (bf16[2048,512]{1,0:T(8,128)(2,1)S(1)}, bf16[2048,512]{1,0:T(8,128)(2,1)}, u32[]{:S(2)}) copy-start(bf16[2048,512]{1,0:T(8,128)(2,1)} %param.12) | copy-start | bytes 6291460
  7.2 88.7 %reduce-scatter.2.cloned.1.call-start = ((), (), s32[]{:S(2)}) async-start(), calls=%async_computation.2 | async-start | bytes 786432 | tf_op jit(solution)/shard_map/reduce_scatter | solution.py:44
  95.9 29.1 %all-to-all-start = ((f32[1,16,32,128]{3,2,0,1:T(8,128)}), f32[1,16,32,128]{3,2,0,1:T(8,128)S(1)}, u32[]{:S(2)}, u32[]{:S(2)}) async-start(f32[1,16,32,128]{3,2,0,1:T(8,128)} %bitcast.30), calls=%async_computation.1 | async-start | bytes 524288 | tf_op jit(solution)/shard_map/all_to_all | solution.py:50
  101.7 23.3 %copy-start.1 = (bf16[2048,256]{1,0:T(8,128)(2,1)S(1)}, bf16[2048,256]{1,0:T(8,128)(2,1)}, u32[]{:S(2)}) copy-start(bf16[2048,256]{1,0:T(8,128)(2,1)} %param.11) | copy-start | bytes 3145732
  101.7 33.9 %copy-start.3 = (s32[2048]{0:T(1024)S(1)}, s32[2048]{0:T(1024)}, u32[]{:S(2)}) copy-start(s32[2048]{0:T(1024)} %param.15) | copy-start | bytes 24580
  125.8 33.2 %copy-start.2 = (f32[32,256]{1,0:T(8,128)}, f32[32,256]{1,0:T(8,128)S(1)}, u32[]{:S(2)}) copy-start(f32[32,256]{1,0:T(8,128)S(1)} %broadcast_multiply_fusion) | copy-start | bytes 98308
Sparse Core Ops, SparseCore 0:
  78.5 17.2 reduce-scatter.1
where the time goes:
time: 166 us
  local copies, waits for them, and re-layouts  60.3 us (36%)
  blocking collectives  28.5 us (17%)
  matrix products  28 us (17%)
  waiting for transfers between devices  17.5 us (11%)
  between operations  14.2 us (9%)
  other arithmetic  11.5 us (7%)
  starting transfers between devices  5.86 us (4%)
    gather x1, local copies, waits for them, and re-layouts, lookup_pool(): jnp.take(table, jnp.clip(local, 0, rows_total - 1), axis=0)  59.4 us
    dot_general x1, matrix products, user_tower(): jnp.dot(user_hidden, user_w2, preferred_element_type=jnp.float32)  23.2 us
    psum x1, blocking collectives, body(): sums, positive = lax.psum((partial_sums[0], partial_sums[1]), 'cand')  18.7 us
    reduce_scatter x1, waiting for transfers between devices, body(): lax.psum_scatter(lookup_pool(own_ids, own_lengths, table, row_base), 'tab...  17.5 us
    all_gather x1, blocking collectives, body(): piece = lax.all_gather(item_emb, ('tab', 'dp'), axis=0, tiled=True)  9.79 us
    reduce_sum x1, other arithmetic, lookup_pool(): jnp.sum(jnp.where(keeping[:, :, None], picked, jnp.float32(0.0)), axis=1)  7.2 us
    all_to_all x1, starting transfers between devices, body(): lax.all_to_all(shaped, ('cand', 'dp'), split_axis=1, concat_axis=0, tiled...  5.82 us
    dot_general x1, matrix products, add_scores(): lax.dot_general(user_emb, piece, (((1,), (1,)), ((), ())), precision=lax....  4.08 us
  transfers between devices with their start and end apart: 2, of which 1 were waited for; matrix products, arithmetic and copies ran while one was open for 14% of the time, Pallas kernels for 0%

commit v1 on v0

v1 whole, which is shorter than its diff:
```python
import functools
import math

import jax
import jax.numpy as jnp
from jax import lax
from jax.experimental import pallas as pl
from jax.experimental.pallas import tpu as pltpu
from jax.sharding import PartitionSpec as P

epsilon = 1e-06
logit_scale = 20.0
MESH = pl.DeviceIdType.MESH
F32 = jnp.float32
BF16 = jnp.bfloat16
VMEM_LIMIT = 60 * 1024 * 1024


def pool_kernel(length, chunks, ids, table, lengths, out, narrow, wide, sems):
    rows, width = table.shape
    items = out.shape[0]
    step = rows // chunks

    def chunk_copy(c):
        part = pl.ds(c * step, step)
        return pltpu.make_async_copy(table.at[part], narrow.at[part], sems.at[c])

    for c in range(chunks):
        chunk_copy(c).start()
    wide[pl.ds(rows, 8), :] = jnp.zeros((8, width), F32)
    piece = min(step, 512)
    for c in range(chunks):
        chunk_copy(c).wait()

        @pl.loop(0, step // piece)
        def _(b):
            part = pl.ds(pl.multiple_of(c * step + b * piece, piece), piece)
            wide[part, :] = narrow[part, :].astype(F32)

    @pl.loop(0, items // 8)
    def _(g):
        first = pl.multiple_of(g * 8, 8)
        for k in range(8):
            terms = [wide[pl.ds(ids[p * items + first + k], 1), :] for p in range(length)]
            while len(terms) > 1:
                terms = [a + b for a, b in zip(terms[::2], terms[1::2])] + (
                    [terms[-1]] if len(terms) % 2 else []
                )
            out[pl.ds(first + k, 1), :] = terms[0]
        block = pl.ds(first, 8)
        out[block, :] = out[block, :] / lengths[block, :]


def pool(table, bag_part, length_part, row_base):
    rows, width = table.shape
    items, length = bag_part.shape
    local = bag_part.T - row_base
    valid = lax.broadcasted_iota(jnp.int32, local.shape, 0) < length_part[None, :]
    keeping = (local >= 0) & (local < rows) & valid
    ids = jnp.where(keeping, local, rows).reshape(-1)
    chunks = math.gcd(rows // 16, 8)
    return pl.pallas_call(
        functools.partial(pool_kernel, length, chunks),
        out_shape=jax.ShapeDtypeStruct((items, width), F32),
        in_specs=[
            pl.BlockSpec(memory_space=pltpu.SMEM),
            pl.BlockSpec(memory_space=pl.ANY),
            pl.BlockSpec(memory_space=pltpu.VMEM),
        ],
        out_specs=pl.BlockSpec(memory_space=pltpu.VMEM),
        scratch_shapes=[
            pltpu.VMEM((rows, width), BF16),
            pltpu.VMEM((rows + 8, width), F32),
            pltpu.SemaphoreType.DMA((chunks,)),
        ],
        compiler_params=pltpu.CompilerParams(vmem_limit_bytes=VMEM_LIMIT),
        name="pool",
    )(ids, table, length_part.astype(F32)[:, None])


def split3(x):
    hi = x.astype(BF16)
    rest = x - hi.astype(F32)
    mid = rest.astype(BF16)
    lo = (rest - mid.astype(F32)).astype(BF16)
    return hi, mid, lo


def split2(x):
    hi = x.astype(BF16)
    return hi, (x - hi.astype(F32)).astype(BF16)


def unit_rows(vectors):
    return vectors * lax.rsqrt(jnp.mean(vectors * vectors, axis=-1, keepdims=True) + epsilon)


def dot(a, b):
    return jnp.dot(a, b, preferred_element_type=F32)


def main_kernel(
    sizes,
    pooled,
    weight,
    features,
    w1,
    w2,
    positives,
    emb_out,
    loss_out,
    arrived,
    joined,
    user_hi,
    user_lo,
    gathered,
    items_flat,
    sums_here,
    sums_all,
    send_a,
    recv_a,
    send_b,
    recv_b,
    send_c,
    recv_c,
):
    num_tab, num_cand, num_dp = sizes
    total = num_tab * num_cand * num_dp
    tables = num_cand * num_dp
    t, c, d = (lax.axis_index(n) for n in ("tab", "cand", "dp"))
    me = (t * num_cand + c) * num_dp + d
    per_block, width = pooled.shape[1:]
    users = features.shape[0]
    hidden = w1.shape[1]
    embed = w2.shape[1]

    def place(index):
        return (index // tables, index // num_dp % num_cand, index % num_dp)

    barrier = pltpu.get_barrier_semaphore()

    @pl.loop(1, total)
    def _(j):
        peer = lax.rem(me + j, total)
        pl.semaphore_signal(barrier, inc=1, device_id=place(peer), device_id_type=MESH)

    pl.semaphore_wait(barrier, total - 1)

    @pl.loop(1, total)
    def _(j):
        peer = lax.rem(me + j, total)
        pltpu.make_async_remote_copy(
            src_ref=pooled.at[peer],
            dst_ref=arrived.at[me],
            send_sem=send_a,
            recv_sem=recv_a,
            device_id=place(peer),
            device_id_type=MESH,
        ).start()

    tile = min(users, 256)
    part_width = min(hidden, 256)

    @pl.loop(0, users // tile)
    def _(u):
        rows = pl.ds(pl.multiple_of(u * tile, tile), tile)
        x = features[rows, :]
        acc = None
        for h in range(0, hidden, part_width):
            z = dot(x, w1[:, h : h + part_width])
            z = z * (0.5 * lax.erf(z * math.sqrt(0.5)) + 0.5)
            term = dot(z.astype(BF16), w2[h : h + part_width, :])
            acc = term if acc is None else acc + term
        hi, lo = split2(unit_rows(acc) * (logit_scale / embed))
        user_hi[rows, :] = hi
        user_lo[rows, :] = lo

    arrived[me] = pooled[me]
    others = pl.ds(0, total - 1)
    pltpu.make_async_copy(arrived.at[others], arrived.at[others], recv_a).wait()
    for f in range(tables):
        block = arrived[f]
        for s in range(1, num_tab):
            block = block + arrived[s * tables + f]
        joined[:, f * width : (f + 1) * width] = block
    hi, mid, lo = split3(joined[...])
    w = weight[...]
    item_emb = unit_rows(dot(lo, w) + dot(mid, w) + dot(hi, w))
    emb_out[...] = item_emb

    slots = num_tab * num_dp
    my_slot = t * num_dp + d

    @pl.loop(1, slots)
    def _(j):
        slot = lax.rem(my_slot + j, slots)
        pltpu.make_async_remote_copy(
            src_ref=emb_out,
            dst_ref=gathered.at[my_slot],
            send_sem=send_b,
            recv_sem=recv_b,
            device_id=(slot // num_dp, c, lax.rem(slot, num_dp)),
            device_id_type=MESH,
        ).start()

    gathered[my_slot] = item_emb
    others_b = pl.ds(0, slots - 1)
    pltpu.make_async_copy(gathered.at[others_b], gathered.at[others_b], recv_b).wait()
    for s in range(slots):
        items_flat[s * per_block : (s + 1) * per_block, :] = gathered[s]
    item_hi, item_lo = split2(items_flat[...])
    count = slots * per_block
    column = min(users, 256)

    @pl.loop(0, users // column)
    def _(u):
        rows = pl.ds(pl.multiple_of(u * column, column), column)
        uh, ul = user_hi[rows, :], user_lo[rows, :]

        def cross(a, b):
            return lax.dot_general(a, b, (((1,), (1,)), ((), ())), preferred_element_type=F32)

        scores = cross(item_lo, uh) + cross(item_hi, ul) + cross(item_hi, uh)
        line = lax.broadcasted_iota(jnp.int32, (count, 1), 0)
        slot = line // per_block
        ids = ((slot // num_dp * num_cand + c) * num_dp + slot % num_dp) * per_block + line % per_block
        sums_here[0:1, rows] = jnp.sum(jnp.exp(scores), axis=0, keepdims=True)
        sums_here[1:2, rows] = jnp.sum(
            jnp.where(ids == positives[:, rows], scores, jnp.float32(0.0)), axis=0, keepdims=True
        )

    @pl.loop(1, num_cand)
    def _(j):
        peer = lax.rem(c + j, num_cand)
        pltpu.make_async_remote_copy(
            src_ref=sums_here,
            dst_ref=sums_all.at[c],
            send_sem=send_c,
            recv_sem=recv_c,
            device_id=(t, peer, d),
            device_id_type=MESH,
        ).start()

    sums_all[c] = sums_here[...]
    others_c = pl.ds(0, num_cand - 1)
    pltpu.make_async_copy(sums_all.at[others_c], sums_all.at[others_c], recv_c).wait()
    both = sums_all[0]
    for s in range(1, num_cand):
        both = both + sums_all[s]
    loss_out[...] = jnp.log(both[0:1, :]) - both[1:2, :]

    pltpu.make_async_copy(pooled.at[others], pooled.at[others], send_a).wait()
    pltpu.make_async_copy(gathered.at[others_b], gathered.at[others_b], send_b).wait()
    pltpu.make_async_copy(sums_all.at[others_c], sums_all.at[others_c], send_c).wait()


def body(
    tables, bag_ids, bag_lengths, item_weight, user_features, user_w1, user_w2, positive_items
):
    sizes = tuple(lax.axis_size(n) for n in ("tab", "cand", "dp"))
    total = math.prod(sizes)
    slots = sizes[0] * sizes[2]
    table = tables[0]
    rows, width = table.shape
    row_base = lax.axis_index("tab") * rows
    pooled = pool(table, bag_ids[0], bag_lengths[0], row_base)
    per_block = pooled.shape[0] // total
    users = user_features.shape[0]
    embed = user_w2.shape[1]
    vmem = pl.BlockSpec(memory_space=pltpu.VMEM)
    item_emb, loss = pl.pallas_call(
        functools.partial(main_kernel, sizes),
        out_shape=(
            jax.ShapeDtypeStruct((per_block, embed), F32),
            jax.ShapeDtypeStruct((1, users), F32),
        ),
        in_specs=[vmem] * 6,
        out_specs=(vmem, vmem),
        scratch_shapes=[
            pltpu.VMEM((total, per_block, width), F32),
            pltpu.VMEM((per_block, item_weight.shape[0]), F32),
            pltpu.VMEM((users, embed), BF16),
            pltpu.VMEM((users, embed), BF16),
            pltpu.VMEM((slots, per_block, embed), F32),
            pltpu.VMEM((slots * per_block, embed), F32),
            pltpu.VMEM((2, users), F32),
            pltpu.VMEM((sizes[1], 2, users), F32),
        ]
        + [pltpu.SemaphoreType.DMA] * 6,
        compiler_params=pltpu.CompilerParams(
            collective_id=0, has_side_effects=True, vmem_limit_bytes=VMEM_LIMIT
        ),
        name="towers",
    )(
        pooled.reshape(total, per_block, width),
        item_weight,
        user_features,
        user_w1,
        user_w2,
        positive_items[None, :],
    )
    return (item_emb, loss[0])


def solution(mesh):
    placed = (
        P(("cand", "dp"), "tab", None),
        P(("cand", "dp"), None, None),
        P(("cand", "dp"), None),
        P(),
        P(("tab", "dp"), None),
        P(),
        P(),
        P(("tab", "dp")),
    )
    return jax.shard_map(
        body,
        mesh=mesh,
        in_specs=placed,
        out_specs=(P(("tab", "cand", "dp"), None), P(("tab", "dp"))),
        check_vma=False,
    )
```

time: 166 us -> 63 us (0.38)
  Pallas kernels: 0 us -> 56.1 us
  local copies, waits for them, and re-layouts: 60.3 us -> 4.35 us
  blocking collectives: 28.5 us -> 0 us
  matrix products: 28 us -> 0 us
  waiting for transfers between devices: 17.5 us -> 0 us
  between operations: 14.2 us -> 0.66 us
  other arithmetic: 11.5 us -> 1.55 us
  starting transfers between devices: 5.86 us -> 0 us
    gather x1 -> x0, local copies, waits for them, and re-layouts: 59.4 us -> none  [lookup_pool(): jnp.take(table, jnp.clip(local, 0, rows_total - 1), axis=0)]
    pallas_call x0 -> x2, Pallas kernels: none -> 56.1 us  [the longest x1 35.6 us: body(): pl.pallas_call(functools.partial(main_kernel, sizes), out_shape=(jax.Shap...]
    dot_general x3 -> x0, matrix products: 28 us -> none  [the longest x1 23.2 us: user_tower(): jnp.dot(user_hidden, user_w2, preferred_element_type=jnp.float32)]
    psum x1 -> x0, blocking collectives: 18.7 us -> none  [body(): sums, positive = lax.psum((partial_sums[0], partial_sums[1]), 'cand')]
    reduce_scatter x1 -> x0, waiting for transfers between devices: 17.5 us -> none  [body(): lax.psum_scatter(lookup_pool(own_ids, own_lengths, table, row_base), 'tab...]
    all_gather x1 -> x0, blocking collectives: 9.79 us -> none  [body(): piece = lax.all_gather(item_emb, ('tab', 'dp'), axis=0, tiled=True)]
    reduce_sum x1 -> x0, other arithmetic: 7.2 us -> none  [lookup_pool(): jnp.sum(jnp.where(keeping[:, :, None], picked, jnp.float32(0.0)), axis=1)]
    all_to_all x1 -> x0, starting transfers between devices: 5.82 us -> none  [body(): lax.all_to_all(shaped, ('cand', 'dp'), split_axis=1, concat_axis=0, tiled...]
  transfers between devices with their start and end apart: 2 -> 0, of which waited for: 1 -> 0; matrix products, arithmetic and copies ran while one was open for 14% -> 0% of each run, Pallas kernels for 0% -> 0%
where the time goes in v1:
time: 63 us; the launch traced here: 62.6 us
  Pallas kernels  56.1 us (89%)
  local copies, waits for them, and re-layouts  4.35 us (7%)
  other arithmetic  1.55 us (2%)
  between operations  0.66 us (1%)
    pallas_call x1, Pallas kernels, body(): pl.pallas_call(functools.partial(main_kernel, sizes), out_shape=(jax.Shap...  35.6 us
    pallas_call x1, Pallas kernels, pool(): pl.pallas_call(functools.partial(pool_kernel, length, chunks), out_shape=...  20.5 us
    unnamed x3, local copies, waits for them, and re-layouts  3.31 us

profile of v1, /device:TPU:0, one launch (start us, length us, event | category | flops | bytes accessed | tf_op | source)
XLA Modules:
  0.0 62.6 jit_solution(15303697826811492428)
XLA Ops:
  0.6 0.7 %convert_bitcast_fusion = f32[1024,1]{0,1:T(1,128)S(1)} fusion(s32[1,1024]{1,0:T(1,128)} %param.10), kind=kLoop, calls=%fused_computation.7 | loop fusion | flops 1024 | bytes 8192 | tf_op jit(solution)/shard_map/convert_element_type | solution.py:78
  1.3 0.9 %fusion = s32[2,8,8,128]{3,2,1,0:T(8,128)S(1)} fusion(s32[1,1024,16]{1,2,0:T(8,128)} %param.9, s32[1024]{0:T(1024)} %bitcast.27, s32[]{:T(128)S(6)} %mul.3), kind=kLoop, calls=%fused_computation.3 | loop fusion | flops 114688 | bytes 135172
  2.2 0.6 %copy.11 = s32[2,8,8,128]{3,1,2,0:T(8,128)} copy(s32[2,8,8,128]{3,2,1,0:T(8,128)S(1)} %fusion) | data formatting | bytes 131072
  2.8 1.0 %copy.10.lengths = f32[1024,1]{1,0:T(8,128)} copy(f32[1024,1]{0,1:T(1,128)S(1)} %convert_bitcast_fusion) | data formatting | bytes 8192 | tf_op jit(solution)/shard_map/convert_element_type | solution.py:78
  3.9 20.5 %pool.1 = f32[1024,128]{1,0:T(8,128)} custom-call(s32[16384]{0:T(1024)} %bitcast.26, bf16[32768,128]{1,0:T(8,128)(2,1)} %bitcast.24, f32[1024,1]{1,0:T(8,128)} %copy.10.lengths), custom_call_target="tpu_custom_call" | custom-call | tf_op jit(solution)/shard_map/pool/pallas_call | solution.py:62
  24.4 35.6 %towers.1 = (f32[32,256]{1,0:T(8,128)}, f32[1,2048]{1,0:T(1,128)}) custom-call(f32[32,32,128]{2,1,0:T(8,128)} %bitcast.25, bf16[2048,256]{1,0:T(8,128)(2,1)} %weight.1, bf16[2048,512]{1,0:T(8,128)(2,1)} %features.1, bf16[512,1024]{1,0:T(8,128)(2,1)} %w1.1, bf16[1024,256]{1,0:T(8,128)(2,1)} %w2.1, s32[1,2048]{1,0:T(1,128)} %bitcast.28), custom_call_target="tpu_custom_call" | custom-call | tf_op jit(solution)/shard_map/towers/pallas_call | solution.py:271
  60.0 1.4 %copy.14 = f32[32,256]{1,0:T(8,128)} copy(f32[32,256]{1,0:T(8,128)} %get-tuple-element.8) | data formatting | bytes 65536
  61.3 1.3 %copy.15 = f32[2048]{0:T(1024)} copy(f32[2048]{0:T(1024)} %bitcast.29) | data formatting | bytes 16384

commit v2 on v1

--- a/solution.py
+++ b/solution.py
@@ -16,68 +16,6 @@
 VMEM_LIMIT = 60 * 1024 * 1024
 
 
-def pool_kernel(length, chunks, ids, table, lengths, out, narrow, wide, sems):
-    rows, width = table.shape
-    items = out.shape[0]
-    step = rows // chunks
-
-    def chunk_copy(c):
-        part = pl.ds(c * step, step)
-        return pltpu.make_async_copy(table.at[part], narrow.at[part], sems.at[c])
-
-    for c in range(chunks):
-        chunk_copy(c).start()
-    wide[pl.ds(rows, 8), :] = jnp.zeros((8, width), F32)
-    piece = min(step, 512)
-    for c in range(chunks):
-        chunk_copy(c).wait()
-
-        @pl.loop(0, step // piece)
-        def _(b):
-            part = pl.ds(pl.multiple_of(c * step + b * piece, piece), piece)
-            wide[part, :] = narrow[part, :].astype(F32)
-
-    @pl.loop(0, items // 8)
-    def _(g):
-        first = pl.multiple_of(g * 8, 8)
-        for k in range(8):
-            terms = [wide[pl.ds(ids[p * items + first + k], 1), :] for p in range(length)]
-            while len(terms) > 1:
-                terms = [a + b for a, b in zip(terms[::2], terms[1::2])] + (
-                    [terms[-1]] if len(terms) % 2 else []
-                )
-            out[pl.ds(first + k, 1), :] = terms[0]
-        block = pl.ds(first, 8)
-        out[block, :] = out[block, :] / lengths[block, :]
-
-
-def pool(table, bag_part, length_part, row_base):
-    rows, width = table.shape
-    items, length = bag_part.shape
-    local = bag_part.T - row_base
-    valid = lax.broadcasted_iota(jnp.int32, local.shape, 0) < length_part[None, :]
-    keeping = (local >= 0) & (local < rows) & valid
-    ids = jnp.where(keeping, local, rows).reshape(-1)
-    chunks = math.gcd(rows // 16, 8)
-    return pl.pallas_call(
-        functools.partial(pool_kernel, length, chunks),
-        out_shape=jax.ShapeDtypeStruct((items, width), F32),
-        in_specs=[
-            pl.BlockSpec(memory_space=pltpu.SMEM),
-            pl.BlockSpec(memory_space=pl.ANY),
-            pl.BlockSpec(memory_space=pltpu.VMEM),
-        ],
-        out_specs=pl.BlockSpec(memory_space=pltpu.VMEM),
-        scratch_shapes=[
-            pltpu.VMEM((rows, width), BF16),
-            pltpu.VMEM((rows + 8, width), F32),
-            pltpu.SemaphoreType.DMA((chunks,)),
-        ],
-        compiler_params=pltpu.CompilerParams(vmem_limit_bytes=VMEM_LIMIT),
-        name="pool",
-    )(ids, table, length_part.astype(F32)[:, None])
-
-
 def split3(x):
     hi = x.astype(BF16)
     rest = x - hi.astype(F32)
@@ -101,22 +39,34 @@
 
 def main_kernel(
     sizes,
-    pooled,
+    ids,
+    inverse,
+    table,
+    weight_in,
+    features_in,
+    w1_in,
+    w2_in,
+    positives,
+    emb_out,
+    loss_out,
+    narrow,
+    wide,
     weight,
     features,
     w1,
     w2,
-    positives,
-    emb_out,
-    loss_out,
+    pooled,
     arrived,
     joined,
+    acc,
     user_hi,
     user_lo,
     gathered,
     items_flat,
     sums_here,
     sums_all,
+    load_sems,
+    table_sems,
     send_a,
     recv_a,
     send_b,
@@ -126,16 +76,28 @@
 ):
     num_tab, num_cand, num_dp = sizes
     total = num_tab * num_cand * num_dp
-    tables = num_cand * num_dp
+    groups = num_cand * num_dp
     t, c, d = (lax.axis_index(n) for n in ("tab", "cand", "dp"))
     me = (t * num_cand + c) * num_dp + d
     per_block, width = pooled.shape[1:]
+    items = total * per_block
+    length = ids.shape[0] // items
+    rows, _ = table.shape
     users = features.shape[0]
     hidden = w1.shape[1]
     embed = w2.shape[1]
+    tile = acc.shape[0]
+    part_width = min(hidden, 256)
+    parts = hidden // part_width
+    tiles = users // tile
+    chunks = table_sems.shape[0]
+    steps = (tiles - chunks) * parts
+    blocks_step = total // steps
+    items_step = items // steps
+    chunk = rows // chunks
 
     def place(index):
-        return (index // tables, index // num_dp % num_cand, index % num_dp)
+        return (index // groups, index // num_dp % num_cand, index % num_dp)
 
     barrier = pltpu.get_barrier_semaphore()
 
@@ -144,44 +106,108 @@
         peer = lax.rem(me + j, total)
         pl.semaphore_signal(barrier, inc=1, device_id=place(peer), device_id_type=MESH)
 
+    loads = [
+        pltpu.make_async_copy(a, b, load_sems.at[i])
+        for i, (a, b) in enumerate(
+            ((w1_in, w1), (w2_in, w2), (features_in, features), (weight_in, weight))
+        )
+    ]
+
+    def chunk_copy(n):
+        part = pl.ds(pl.multiple_of(n * chunk, chunk), chunk)
+        return pltpu.make_async_copy(table.at[part], narrow.at[part], table_sems.at[n])
+
+    for load in loads[:3]:
+        load.start()
+    for n in range(chunks):
+        chunk_copy(n).start()
+    loads[3].start()
+    wide[pl.ds(rows, 8), :] = jnp.zeros((8, width), F32)
+    for load in loads[:3]:
+        load.wait()
+
+    def tower_part(x, w1_part, w2_part):
+        z = dot(x, w1_part)
+        z = z * (0.5 * lax.erf(z * math.sqrt(0.5)) + 0.5)
+        return dot(z.astype(BF16), w2_part)
+
+    def keep_user(user_rows, pre):
+        hi, lo = split2(unit_rows(pre) * (logit_scale / embed))
+        user_hi[user_rows, :] = hi
+        user_lo[user_rows, :] = lo
+
+    @pl.loop(0, chunks)
+    def _(n):
+        user_rows = pl.ds(pl.multiple_of(n * tile, tile), tile)
+        chunk_copy(n).wait()
+        part = pl.ds(pl.multiple_of(n * chunk, chunk), chunk)
+        wide[part, :] = narrow[part, :].astype(F32)
+        x = features[user_rows, :]
+        pre = None
+        for h in range(0, hidden, part_width):
+            term = tower_part(x, w1[:, h : h + part_width], w2[h : h + part_width, :])
+            pre = term if pre is None else pre + term
+        keep_user(user_rows, pre)
+
     pl.semaphore_wait(barrier, total - 1)
 
-    @pl.loop(1, total)
-    def _(j):
-        peer = lax.rem(me + j, total)
+    def send(dest):
         pltpu.make_async_remote_copy(
-            src_ref=pooled.at[peer],
+            src_ref=pooled.at[dest],
             dst_ref=arrived.at[me],
             send_sem=send_a,
             recv_sem=recv_a,
-            device_id=place(peer),
+            device_id=place(dest),
             device_id_type=MESH,
         ).start()
 
-    tile = min(users, 256)
-    part_width = min(hidden, 256)
-
-    @pl.loop(0, users // tile)
-    def _(u):
-        rows = pl.ds(pl.multiple_of(u * tile, tile), tile)
-        x = features[rows, :]
-        acc = None
-        for h in range(0, hidden, part_width):
-            z = dot(x, w1[:, h : h + part_width])
-            z = z * (0.5 * lax.erf(z * math.sqrt(0.5)) + 0.5)
-            term = dot(z.astype(BF16), w2[h : h + part_width, :])
-            acc = term if acc is None else acc + term
-        hi, lo = split2(unit_rows(acc) * (logit_scale / embed))
-        user_hi[rows, :] = hi
-        user_lo[rows, :] = lo
+    my_group = me // blocks_step
+
+    @pl.loop(0, steps)
+    def _(s):
+        @pl.when(s > 0)
+        def _():
+            before = lax.rem(my_group + s, steps)
+            for i in range(blocks_step):
+                send(before * blocks_step + i)
+
+        group = lax.rem(my_group + 1 + s, steps)
+        first = group * items_step
+        for k in range(items_step):
+            terms = [wide[pl.ds(ids[p * items + first + k], 1), :] for p in range(length)]
+            while len(terms) > 1:
+                terms = [a + b for a, b in zip(terms[::2], terms[1::2])] + (
+                    [terms[-1]] if len(terms) % 2 else []
+                )
+            row = terms[0] * inverse[first + k]
+            pooled[group * blocks_step + k // per_block, pl.ds(k % per_block, 1), :] = row
+
+        piece = lax.rem(s, parts)
+        user_rows = pl.ds(pl.multiple_of((chunks + s // parts) * tile, tile), tile)
+        cols = pl.ds(pl.multiple_of(piece * part_width, part_width), part_width)
+        term = tower_part(features[user_rows, :], w1[:, cols], w2[cols, :])
+        acc[...] = jnp.where(piece == 0, jnp.zeros_like(term), acc[...]) + term
+
+        @pl.when(piece == parts - 1)
+        def _():
+            keep_user(user_rows, acc[...])
+
+    for i in range(blocks_step):
+        dest = my_group * blocks_step + i
+        if blocks_step > 1:
+
+            @pl.when(dest != me)
+            def _():
+                send(dest)
 
     arrived[me] = pooled[me]
+    loads[3].wait()
     others = pl.ds(0, total - 1)
     pltpu.make_async_copy(arrived.at[others], arrived.at[others], recv_a).wait()
-    for f in range(tables):
+    for f in range(groups):
         block = arrived[f]
         for s in range(1, num_tab):
-            block = block + arrived[s * tables + f]
+            block = block + arrived[s * groups + f]
         joined[:, f * width : (f + 1) * width] = block
     hi, mid, lo = split3(joined[...])
     w = weight[...]
@@ -262,37 +288,57 @@
     slots = sizes[0] * sizes[2]
     table = tables[0]
     rows, width = table.shape
-    row_base = lax.axis_index("tab") * rows
-    pooled = pool(table, bag_ids[0], bag_lengths[0], row_base)
-    per_block = pooled.shape[0] // total
+    items, length = bag_ids.shape[1:]
+    per_block = items // total
     users = user_features.shape[0]
     embed = user_w2.shape[1]
+    local = bag_ids[0].T - lax.axis_index("tab") * rows
+    valid = lax.broadcasted_iota(jnp.int32, local.shape, 0) < bag_lengths
+    keeping = (local >= 0) & (local < rows) & valid
+    ids = jnp.where(keeping, local, rows).reshape(-1)
+    inverse = 1.0 / bag_lengths[0].astype(F32)
+    tile = 128
+    chunks = users // tile // 2
     vmem = pl.BlockSpec(memory_space=pltpu.VMEM)
+    smem = pl.BlockSpec(memory_space=pltpu.SMEM)
+    anywhere = pl.BlockSpec(memory_space=pl.ANY)
     item_emb, loss = pl.pallas_call(
         functools.partial(main_kernel, sizes),
         out_shape=(
             jax.ShapeDtypeStruct((per_block, embed), F32),
             jax.ShapeDtypeStruct((1, users), F32),
         ),
-        in_specs=[vmem] * 6,
+        in_specs=[smem] * 2 + [anywhere] * 5 + [vmem],
         out_specs=(vmem, vmem),
         scratch_shapes=[
+            pltpu.VMEM((rows, width), BF16),
+            pltpu.VMEM((rows + 8, width), F32),
+            pltpu.VMEM(item_weight.shape, BF16),
+            pltpu.VMEM(user_features.shape, BF16),
+            pltpu.VMEM(user_w1.shape, BF16),
+            pltpu.VMEM(user_w2.shape, BF16),
+            pltpu.VMEM((total, per_block, width), F32),
             pltpu.VMEM((total, per_block, width), F32),
             pltpu.VMEM((per_block, item_weight.shape[0]), F32),
+            pltpu.VMEM((tile, embed), F32),
             pltpu.VMEM((users, embed), BF16),
             pltpu.VMEM((users, embed), BF16),
             pltpu.VMEM((slots, per_block, embed), F32),
             pltpu.VMEM((slots * per_block, embed), F32),
             pltpu.VMEM((2, users), F32),
             pltpu.VMEM((sizes[1], 2, users), F32),
+            pltpu.SemaphoreType.DMA((4,)),
+            pltpu.SemaphoreType.DMA((chunks,)),
         ]
         + [pltpu.SemaphoreType.DMA] * 6,
         compiler_params=pltpu.CompilerParams(
             collective_id=0, has_side_effects=True, vmem_limit_bytes=VMEM_LIMIT
         ),
-        name="towers",
+        name="step",
     )(
-        pooled.reshape(total, per_block, width),
+        ids,
+        inverse,
+        table,
         item_weight,
         user_features,
         user_w1,

time: 63 us -> 62.7 us (level)
  local copies, waits for them, and re-layouts: 4.35 us -> 3.3 us
    pallas_call x1, Pallas kernels: 35.6 us -> 56.2 us  [body(): pl.pallas_call(functools.partial(main_kernel, sizes), out_shape=(jax.Shap...]
    pallas_call x1 -> x0, Pallas kernels: 20.5 us -> none  [pool(): pl.pallas_call(functools.partial(pool_kernel, length, chunks), out_shape=...]
    div x0 -> x1, other arithmetic: none -> 1.29 us  [body(): inverse = 1.0 / bag_lengths[0].astype(F32)]
    convert_element_type x1 -> x0, local copies, waits for them, and re-layouts: 1.04 us -> none  [pool(): length_part.astype(F32)[:, None]]
    convert_element_type x1 -> x0, other arithmetic: 0.69 us -> none  [pool(): length_part.astype(F32)[:, None]]
where the time goes in v2:
time: 62.7 us; the launch traced here: 62.3 us
  Pallas kernels  56.2 us (90%)
  local copies, waits for them, and re-layouts  3.3 us (5%)
  other arithmetic  2.15 us (3%)
  between operations  0.65 us (1%)
    pallas_call x1, Pallas kernels, body(): pl.pallas_call(functools.partial(main_kernel, sizes), out_shape=(jax.Shap...  56.2 us
    unnamed x3, local copies, waits for them, and re-layouts  3.3 us
    div x1, other arithmetic, body(): inverse = 1.0 / bag_lengths[0].astype(F32)  1.29 us

profile of v2, /device:TPU:0, one launch (start us, length us, event | category | flops | bytes accessed | tf_op | source)
XLA Modules:
  0.0 62.3 jit_solution(7598048900320410322)
XLA Ops:
  0.6 0.9 %fusion = s32[2,8,8,128]{3,2,1,0:T(8,128)S(1)} fusion(s32[1,1024,16]{1,2,0:T(8,128)} %param.9, s32[1024]{0:T(1024)} %bitcast.23, s32[]{:T(128)S(6)} %mul.3), kind=kLoop, calls=%fused_computation.3 | loop fusion | flops 114688 | bytes 135172
  1.5 0.6 %copy.10 = s32[2,8,8,128]{3,1,2,0:T(8,128)} copy(s32[2,8,8,128]{3,2,1,0:T(8,128)S(1)} %fusion) | data formatting | bytes 131072
  2.1 1.3 %convert_divide_fusion.inverse = f32[1024]{0:T(1024)} fusion(s32[1024]{0:T(1024)} %bitcast.24), kind=kLoop, calls=%fused_computation.7 | loop fusion | flops 2048 | bytes 8192 | tf_op jit(solution)/shard_map/div | solution.py:299
  3.4 56.2 %step.1 = (f32[32,256]{1,0:T(8,128)}, f32[1,2048]{1,0:T(1,128)}) custom-call(s32[16384]{0:T(1024)} %bitcast.22, f32[1024]{0:T(1024)} %convert_divide_fusion.inverse, bf16[32768,128]{1,0:T(8,128)(2,1)} %bitcast.21, bf16[2048,256]{1,0:T(8,128)(2,1)} %weight_in.1, bf16[2048,512]{1,0:T(8,128)(2,1)} %features_in.1, bf16[512,1024]{1,0:T(8,128)(2,1)} %w1_in.1, ...), custom_call_target="tpu_custom_call" | custom-call | tf_op jit(solution)/shard_map/step/pallas_call | solution.py:305
  59.6 1.4 %copy.13 = f32[32,256]{1,0:T(8,128)} copy(f32[32,256]{1,0:T(8,128)} %get-tuple-element.8) | data formatting | bytes 65536
  61.0 1.3 %copy.14 = f32[2048]{0:T(1024)} copy(f32[2048]{0:T(1024)} %bitcast.25) | data formatting | bytes 16384

commit v3 on v2

--- a/solution.py
+++ b/solution.py
@@ -38,6 +38,15 @@
 
 
 def main_kernel(
+    sizes,
+    length,
+    *refs,
+):
+    ids, refs = refs[:length], refs[length:]
+    run_step(sizes, ids, *refs)
+
+
+def run_step(
     sizes,
     ids,
     inverse,
@@ -81,7 +90,6 @@
     me = (t * num_cand + c) * num_dp + d
     per_block, width = pooled.shape[1:]
     items = total * per_block
-    length = ids.shape[0] // items
     rows, _ = table.shape
     users = features.shape[0]
     hidden = w1.shape[1]
@@ -174,7 +182,7 @@
         group = lax.rem(my_group + 1 + s, steps)
         first = group * items_step
         for k in range(items_step):
-            terms = [wide[pl.ds(ids[p * items + first + k], 1), :] for p in range(length)]
+            terms = [wide[pl.ds(of_place[first + k], 1), :] for of_place in ids]
             while len(terms) > 1:
                 terms = [a + b for a, b in zip(terms[::2], terms[1::2])] + (
                     [terms[-1]] if len(terms) % 2 else []
@@ -295,7 +303,7 @@
     local = bag_ids[0].T - lax.axis_index("tab") * rows
     valid = lax.broadcasted_iota(jnp.int32, local.shape, 0) < bag_lengths
     keeping = (local >= 0) & (local < rows) & valid
-    ids = jnp.where(keeping, local, rows).reshape(-1)
+    ids = jnp.where(keeping, local, rows)
     inverse = 1.0 / bag_lengths[0].astype(F32)
     tile = 128
     chunks = users // tile // 2
@@ -303,12 +311,12 @@
     smem = pl.BlockSpec(memory_space=pltpu.SMEM)
     anywhere = pl.BlockSpec(memory_space=pl.ANY)
     item_emb, loss = pl.pallas_call(
-        functools.partial(main_kernel, sizes),
+        functools.partial(main_kernel, sizes, length),
         out_shape=(
             jax.ShapeDtypeStruct((per_block, embed), F32),
             jax.ShapeDtypeStruct((1, users), F32),
         ),
-        in_specs=[smem] * 2 + [anywhere] * 5 + [vmem],
+        in_specs=[smem] * (length + 1) + [anywhere] * 5 + [vmem],
         out_specs=(vmem, vmem),
         scratch_shapes=[
             pltpu.VMEM((rows, width), BF16),
@@ -336,7 +344,7 @@
         ),
         name="step",
     )(
-        ids,
+        *[ids[p] for p in range(length)],
         inverse,
         table,
         item_weight,

time: 62.7 us -> 59.5 us (0.949)
  Pallas kernels: 56.2 us -> 53 us
    pallas_call x1, Pallas kernels: 56.2 us -> 53 us  [body(): pl.pallas_call(functools.partial(main_kernel, sizes, length), out_shape=(...]
    select_n x0 -> x1, other arithmetic: none -> 0.86 us  [body(): ids = jnp.where(keeping, local, rows)]
    unnamed x1 -> x0, other arithmetic: 0.86 us -> none
    slice x0 -> x1, local copies, waits for them, and re-layouts: none -> 0.67 us  [body(): ids[p]]
    unnamed x3 -> x2, local copies, waits for them, and re-layouts: 3.3 us -> 2.67 us
where the time goes in v3:
time: 59.5 us; the launch traced here: 59.1 us
  Pallas kernels  53 us (89%)
  local copies, waits for them, and re-layouts  3.34 us (6%)
  other arithmetic  2.15 us (4%)
  between operations  0.65 us (1%)
    pallas_call x1, Pallas kernels, body(): pl.pallas_call(functools.partial(main_kernel, sizes, length), out_shape=(...  53 us
    unnamed x2, local copies, waits for them, and re-layouts  2.67 us
    div x1, other arithmetic, body(): inverse = 1.0 / bag_lengths[0].astype(F32)  1.28 us

profile of v3, /device:TPU:0, one launch (start us, length us, event | category | flops | bytes accessed | tf_op | source)
XLA Modules:
  0.0 59.1 jit_solution(2216253437816136074)
XLA Ops:
  0.6 0.9 %bitcast_select_fusion = s32[16,1024]{1,0:T(8,128)S(1)} fusion(s32[1,1024,16]{1,2,0:T(8,128)} %param.9, s32[1024]{0:T(1024)} %bitcast.49, s32[]{:T(128)S(6)} %mul.3), kind=kLoop, calls=%fused_computation | loop fusion | flops 114688 | bytes 135172 | tf_op jit(solution)/shard_map/jit(_where)/select_n | solution.py:306
  1.5 0.7 %fusion.2 = (s32[1,1024]{1,0:T(1,128)}, s32[1,1024]{1,0:T(1,128)}, s32[1,1024]{1,0:T(1,128)}, s32[1,1024]{1,0:T(1,128)}, s32[1,1024]{1,0:T(1,128)}, /*index=5*/s...) fusion(s32[16,1024]{1,0:T(8,128)S(1)} %bitcast_select_fusion), kind=kLoop, calls=%fused_computation.7 | loop fusion | bytes 131072 | tf_op jit(solution)/shard_map/slice | solution.py:347
  2.2 1.3 %convert_divide_fusion.refs_16_ = f32[1024]{0:T(1024)} fusion(s32[1024]{0:T(1024)} %bitcast.50), kind=kLoop, calls=%fused_computation.6 | loop fusion | flops 2048 | bytes 8192 | tf_op jit(solution)/shard_map/div | solution.py:307
  3.5 53.0 %step.1 = (f32[32,256]{1,0:T(8,128)}, f32[1,2048]{1,0:T(1,128)}) custom-call(s32[1024]{0:T(1024)} %bitcast.48, s32[1024]{0:T(1024)} %bitcast.47, s32[1024]{0:T(1024)} %bitcast.46, s32[1024]{0:T(1024)} %bitcast.45, s32[1024]{0:T(1024)} %bitcast.44, s32[1024]{0:T(1024)} %bitcast.43, s32[1024]{0:T(1024)} %bitcast.42, s32[1024]{0:T(1024)} %bitcast.41, ...), custom_call_target="tpu_custom_call" | custom-call | tf_op jit(solution)/shard_map/step/pallas_call | solution.py:313
  56.5 1.4 %copy.12 = f32[32,256]{1,0:T(8,128)} copy(f32[32,256]{1,0:T(8,128)} %get-tuple-element.24) | data formatting | bytes 65536
  57.8 1.3 %copy.13 = f32[2048]{0:T(1024)} copy(f32[2048]{0:T(1024)} %bitcast.51) | data formatting | bytes 16384
